TPU v7x, 32 devices: a whole 2x2x4 slice. The times are simulated.
32 devices in a mesh: rep: 4 (over z), tp: 8 (over y, x, core).
Axes of the slice: x: 2, y: 2, z: 4, core: 2. Of those that a mesh axis runs over, the one named last changes fastest.
Arguments:
- attn: bfloat16 [3072, 4096], P('rep', 'tp'), parts along dimension 0, may hold values from -6 to 6
- output_weight: bfloat16 [4096, 8192], P(None, 'tp'), may hold values from -0.09375 to 0.09375
- adapter_down_weight: bfloat16 [8, 64, 4096], P('tp'), may hold values from -0.09375 to 0.09375
- adapter_up_weight: bfloat16 [8, 64, 8192], P('tp'), may hold values from -0.75 to 0.75
- block_adapter_index: int32 [24], P('rep'), parts along dimension 0, may hold values from 0 to 7
- adapter_page_table: int32 [8], replicated, may hold values from 0 to 7, each once
Outputs:
- projected: bfloat16 [3072, 8192], P('rep', 'tp'), parts along dimension 0
There are 4 independent parts, one for each index of `rep`. A program takes and returns all parts, laid end to end along the dimension named above; an argument that names none is the same for every part. Nothing has to cross between parts.
Inputs may be any that keep to these rules, and one draw needn't show every extreme that they name: adapter_page_table is a permutation; adapter a is stored on tp device adapter_page_table[a] (each device holds exactly one adapter), and row adapter_page_table[a] of adapter_down_weight and adapter_up_weight holds it. `block_adapter_index`: the adapter used by all 128 tokens of a block.
All inputs are finite; a program needn't handle non-finite values.
Results may differ from a plain program's by a relative error of at most 0.0046.
Values may be sent and summed in bfloat16 or wider, within the bound.
A program may use at most 64 MiB of HBM per device.

v0:
```python
import jax
import jax.numpy as jnp
from jax import lax
from jax.sharding import PartitionSpec as P

adapter_scale = 2.0


def shards(
    attn,
    output_weight,
    adapter_down_weight,
    adapter_up_weight,
    block_adapter_index,
    adapter_page_table,
):
    tokens = attn.shape[0]
    blocks = block_adapter_index.shape[0]
    block_rows = tokens // blocks
    page_slot_count = adapter_down_weight.shape[0]
    pool_size = adapter_page_table.shape[0]
    width_out = output_weight.shape[1]
    position = lax.axis_index("tp")
    matches = block_adapter_index[:, None] == jnp.arange(pool_size, dtype=jnp.int32)[None, :]
    block_page_index = jnp.sum(jnp.where(matches, adapter_page_table[None, :], 0), axis=1)
    up_weight_columns = lax.all_to_all(
        adapter_up_weight, "tp", split_axis=2, concat_axis=0, tiled=True
    )
    block_up = up_weight_columns[block_page_index]
    shard_piece = lax.all_gather(attn, "tp", axis=1, tiled=True)
    base_output = jnp.dot(shard_piece, output_weight, preferred_element_type=jnp.float32)
    row_blocks = shard_piece.reshape(blocks, block_rows, shard_piece.shape[1])
    base_output, side_sum = (
        base_output,
        jnp.einsum(
            "btf,srf->bsrt", row_blocks, adapter_down_weight, preferred_element_type=jnp.float32
        ),
    )
    own_pages = position * page_slot_count + jnp.arange(page_slot_count, dtype=jnp.int32)
    owned = (block_page_index[:, None] == own_pages[None, :]).astype(jnp.float32)
    local_term = jnp.sum(owned[:, :, None, None] * side_sum, axis=1)
    shrunk = lax.psum(local_term.astype(jnp.bfloat16), "tp")
    adapter_output = jnp.einsum(
        "brt,brc->btc", shrunk, block_up, preferred_element_type=jnp.float32
    )
    adapter_output = adapter_output.reshape(tokens, width_out)
    return (base_output + adapter_scale * adapter_output).astype(jnp.bfloat16)


def solution(mesh):
    return jax.shard_map(
        shards,
        mesh=mesh,
        in_specs=(
            P("rep", "tp"),
            P(None, "tp"),
            P("tp", None, None),
            P("tp", None, None),
            P("rep"),
            P(),
        ),
        out_specs=P("rep", "tp"),
        check_vma=False,
    )
```

profile of v0, /device:TPU:0, one launch (start us, length us, event | category | flops | bytes accessed | tf_op | source)
XLA Modules:
  0.0 150.3 jit_solution(16534256131757500711)
XLA Ops:
  6.5 0.0 copy-start
  6.5 0.0 all-gather.2.cloned.1.call-start
  6.5 0.7 all-gather.2.cloned.1.call-update
  7.3 9.2 %copy.11 = bf16[1,64,8192]{1,0,2:T(2,128)(2,1)} copy(bf16[1,64,8192]{2,1,0:T(8,128)(2,1)} %param.9) | data formatting | bytes 2097152 | tf_op args[3]
  16.4 0.5 broadcast.42
  16.9 45.3 %reduce = bf16[8192,64]{1,0:T(8,128)(2,1)S(1)} reduce(bf16[8192,1,64]{2,1,0:T(2,128)(2,1)} %bitcast.36, bf16[]{:T(256)} %broadcast.42), dimensions={1}, to_apply=%bitcast.29.reduce_sub_computation | reduce | bytes 2097154
  62.2 0.0 copy-start.1
  62.2 0.0 copy-start.2
  62.2 2.7 %reshape.51 = bf16[8,2,32768]{2,1,0:T(2,128)(2,1)} reshape(bf16[8192,64]{1,0:T(8,128)(2,1)S(1)} %reduce) | data formatting | bytes 2097152
  64.9 5.2 %all-to-all-start = ((bf16[8,2,32768]{2,1,0:T(2,128)(2,1)}), bf16[8,2,32768]{2,1,0:T(2,128)(2,1)S(1)}, u32[]{:S(2)}, u32[]{:S(2)}) async-start(bf16[8,2,32768]{2,1,0:T(2,128)(2,1)} %reshape.51), calls=%async_computation | async-start | bytes 2097152 | tf_op jit(solution)/shard_map/all_to_all | solution.py:26
  70.1 0.2 all-reduce.2.cloned.1.call-start
  70.3 0.0 copy-done.1
  70.3 0.0 copy-done.2
  70.4 0.2 select_reduce_fusion
  70.6 0.0 all-gather.2.cloned.1.call-done
  70.6 0.0 copy-done
  70.6 5.5 %fusion.3 = bf16[6,64,128]{2,1,0:T(8,128)(2,1)} fusion(bf16[6,128,4096]{2,1,0:T(8,128)(2,1)} %bitcast.39, bf16[1,64,4096]{2,1,0:T(8,128)(2,1)S(1)} %copy-done, f32[6]{0:T(128)S(1)} %compare_convert_fusion), kind=kOutput, calls=%fused_computation.7 | convolution fusion | flops 402751488 | bytes 6914072 | tf_op jit(solution)/shard_map/btf,srf->bsrt/dot_general | solution.py:35
  76.0 0.0 all-reduce.2.cloned.1.call-update
  76.1 9.4 %all-to-all-done = bf16[8,2,32768]{2,1,0:T(2,128)(2,1)S(1)} async-done(((bf16[8,2,32768]{2,1,0:T(2,128)(2,1)}), bf16[8,2,32768]{2,1,0:T(2,128)(2,1)S(1)}, u32[]{:S(2)}, u32[]{:S(2)}) %all-to-all-start) | async-done | bytes 1048608 | tf_op jit(solution)/shard_map/all_to_all | solution.py:26
  85.5 4.3 %reshape.52 = bf16[8192,1,64]{2,1,0:T(2,128)(2,1)} reshape(bf16[8,2,32768]{2,1,0:T(2,128)(2,1)S(1)} %all-to-all-done) | data formatting | bytes 2097152
  89.9 2.5 %copy.16 = bf16[1,64,8192]{1,2,0:T(8,128)(2,1)S(1)} copy(bf16[1,64,8192]{1,0,2:T(2,128)(2,1)} %bitcast.37) | data formatting | bytes 2097152
  92.3 1.6 %copy.13 = bf16[1,64,8,1024]{3,1,2,0:T(8,128)(2,1)} copy(bf16[1,64,8,1024]{1,3,2,0:T(8,128)(2,1)S(1)} %bitcast.38) | data formatting | bytes 2097152 | tf_op jit(solution)/shard_map/all_to_all | solution.py:26
  93.9 1.8 %gather_fusion = bf16[6,64,1024]{2,1,0:T(8,128)(2,1)S(1)} fusion(bf16[8,64,1024]{2,1,0:T(8,128)(2,1)} %bitcast.40, s32[1024]{0:T(1024)S(1)} %pad_clamp_fusion), kind=kCustom, calls=%fused_computation | custom fusion | bytes 1572888 | tf_op jit(solution)/shard_map/gather | solution.py:29
  95.8 34.1 %all-reduce.2.cloned.1.call-done = bf16[6,64,128]{2,1,0:T(8,128)(2,1)} async-done(((bf16[6,64,128]{2,1,0:T(8,128)(2,1)}), bf16[6,64,128]{2,1,0:T(8,128)(2,1)}) %all-reduce.2.cloned.1.call-update) | async-done | bytes 98320 | tf_op jit(solution)/shard_map/psum | solution.py:42
  129.9 1.5 %convolution_multiply_fusion = f32[6,128,1024]{2,1,0:T(8,128)S(1)} fusion(bf16[6,64,128]{2,1,0:T(8,128)(2,1)} %all-reduce.2.cloned.1.call-done, bf16[6,64,1024]{2,1,0:T(8,128)(2,1)S(1)} %gather_fusion), kind=kOutput, calls=%fused_computation.3 | convolution fusion | flops 101449728 | bytes 4030464 | tf_op jit(solution)/shard_map/brt,brc->btc/dot_general | solution.py:43
  131.4 12.1 %fusion = bf16[768,1024]{1,0:T(8,128)(2,1)} fusion(f32[6,128,1024]{2,1,0:T(8,128)S(1)} %convolution_multiply_fusion, bf16[768,4096]{1,0:T(8,128)(2,1)} %all-gather.2.cloned.1.call-done, bf16[4096,1024]{1,0:T(8,128)(2,1)} %param.7), kind=kOutput, calls=%fused_computation.2 | convolution fusion | flops 6444023808 | bytes 19398656 | tf_op jit(solution)/shard_map/dot_general | solution.py:31
  (3 shorter events, 0.0 us)
Async XLA Ops:
  6.5 64.1 %copy-start = (bf16[1,64,4096]{2,1,0:T(8,128)(2,1)S(1)}, bf16[1,64,4096]{2,1,0:T(8,128)(2,1)}, u32[]{:S(2)}) copy-start(bf16[1,64,4096]{2,1,0:T(8,128)(2,1)} %param.8) | copy-start | bytes 1572868
  6.5 64.0 %all-gather.2.cloned.1.call-start = ((), (), s32[]{:S(2)}) async-start(), calls=%async_computation.1 | async-start | bytes 7077888 | tf_op jit(solution)/shard_map/all_gather | solution.py:30
  62.2 8.1 %copy-start.1 = (s32[8]{0:T(128)S(1)}, s32[8]{0:T(128)}, u32[]{:S(2)}) copy-start(s32[8]{0:T(128)} %param.11) | copy-start | bytes 100
  62.2 8.1 %copy-start.2 = (s32[6]{0:T(128)S(1)}, s32[6]{0:T(128)}, u32[]{:S(2)}) copy-start(s32[6]{0:T(128)} %param.10) | copy-start | bytes 76
  64.9 20.6 %all-to-all-start = ((bf16[8,2,32768]{2,1,0:T(2,128)(2,1)}), bf16[8,2,32768]{2,1,0:T(2,128)(2,1)S(1)}, u32[]{:S(2)}, u32[]{:S(2)}) async-start(bf16[8,2,32768]{2,1,0:T(2,128)(2,1)} %reshape.51), calls=%async_computation | async-start | bytes 2097152 | tf_op jit(solution)/shard_map/all_to_all | solution.py:26
  70.1 59.7 %all-reduce.2.cloned.1.call-start = ((), (), s32[]{:S(2)}) async-start(), calls=%async_computation.2 | async-start | bytes 196608 | tf_op jit(solution)/shard_map/psum | solution.py:42
Sparse Core Ops, SparseCore 0:
  9.2 49.2 all-gather.1
  76.2 53.6 all-reduce.1
where the time goes:
time: 151 us; the launch traced here: 150 us
  other arithmetic  45.5 us (30%)
  waiting for transfers between devices  44.3 us (29%)
  local copies, waits for them, and re-layouts  22.6 us (15%)
  matrix products  19.1 us (13%)
  between operations  13.5 us (9%)
  starting transfers between devices  5.45 us (4%)
    unnamed x1, other arithmetic  45.3 us
    psum x1, waiting for transfers between devices, shards(): shrunk = lax.psum(local_term.astype(jnp.bfloat16), 'tp')  34.1 us
    unnamed x11, local copies, waits for them, and re-layouts  19.2 us
    dot_general x1, matrix products, shards(): jnp.dot(shard_piece, output_weight, preferred_element_type=jnp.float32)  12.1 us
    all_to_all x1, waiting for transfers between devices, shards(): lax.all_to_all(adapter_up_weight, 'tp', split_axis=2, concat_axis=0, tile...  9.44 us
    dot_general x1, matrix products, shards(): jnp.einsum('btf,srf->bsrt', row_blocks, adapter_down_weight, preferred_el...  5.45 us
    all_to_all x1, starting transfers between devices, shards(): lax.all_to_all(adapter_up_weight, 'tp', split_axis=2, concat_axis=0, tile...  5.23 us
  transfers between devices with their start and end apart: 3, of which 2 were waited for; matrix products, arithmetic and copies ran while one was open for 49% of the time, Pallas kernels for 0%

commit v1 on v0

--- a/solution.py
+++ b/solution.py
@@ -23,8 +23,11 @@
     position = lax.axis_index("tp")
     matches = block_adapter_index[:, None] == jnp.arange(pool_size, dtype=jnp.int32)[None, :]
     block_page_index = jnp.sum(jnp.where(matches, adapter_page_table[None, :], 0), axis=1)
-    up_weight_columns = lax.all_to_all(
-        adapter_up_weight, "tp", split_axis=2, concat_axis=0, tiled=True
+    up_weight_columns = jnp.concatenate(
+        lax.all_to_all(
+            jnp.stack(jnp.split(adapter_up_weight, lax.axis_size("tp"), axis=2)), "tp", 0, 0
+        ),
+        axis=0,
     )
     block_up = up_weight_columns[block_page_index]
     shard_piece = lax.all_gather(attn, "tp", axis=1, tiled=True)

time: 151 us -> 145 us (0.960)
  waiting for transfers between devices: 44.3 us -> 93.2 us
  other arithmetic: 45.5 us -> 0.87 us
  local copies, waits for them, and re-layouts: 22.6 us -> 13.2 us
    unnamed x1 -> x0, other arithmetic: 45.3 us -> none
    all_gather x1, waiting for transfers between devices: 0.02 us -> 40.9 us  [shards(): shard_piece = lax.all_gather(attn, 'tp', axis=1, tiled=True)]
    psum x1, waiting for transfers between devices: 34.1 us -> 51.6 us  [shards(): shrunk = lax.psum(local_term.astype(jnp.bfloat16), 'tp')]
    all_to_all x1, waiting for transfers between devices: 9.44 us -> 0.01 us  [shards(): lax.all_to_all(jnp.stack(jnp.split(adapter_up_weight, lax.axis_size('tp')...]
    unnamed x11 -> x9, local copies, waits for them, and re-layouts: 19.2 us -> 11 us
    all_to_all x1 -> x0, local copies, waits for them, and re-layouts: 1.61 us -> none  [shards(): lax.all_to_all(adapter_up_weight, 'tp', split_axis=2, concat_axis=0, tile...]
    another operation x0 -> x1, local copies, waits for them, and re-layouts: none -> 1.58 us  [shards(): jnp.stack(jnp.split(adapter_up_weight, lax.axis_size('tp'), axis=2))]
  transfers between devices with their start and end apart: 3 -> 3, of which waited for: 2 -> 2; matrix products, arithmetic and copies ran while one was open for 49% -> 13% of each run, Pallas kernels for 0% -> 0%
where the time goes in v1:
time: 145 us
  waiting for transfers between devices  93.2 us (64%)
  matrix products  19 us (13%)
  between operations  13.4 us (9%)
  local copies, waits for them, and re-layouts  13.2 us (9%)
  starting transfers between devices  5.25 us (4%)
    psum x1, waiting for transfers between devices, shards(): shrunk = lax.psum(local_term.astype(jnp.bfloat16), 'tp')  51.6 us
    all_gather x1, waiting for transfers between devices, shards(): shard_piece = lax.all_gather(attn, 'tp', axis=1, tiled=True)  40.9 us
    dot_general x1, matrix products, shards(): jnp.dot(shard_piece, output_weight, preferred_element_type=jnp.float32)  12.1 us
    unnamed x9, local copies, waits for them, and re-layouts  11 us
    dot_general x1, matrix products, shards(): jnp.einsum('btf,srf->bsrt', row_blocks, adapter_down_weight, preferred_el...  5.45 us
    all_to_all x1, starting transfers between devices, shards(): lax.all_to_all(jnp.stack(jnp.split(adapter_up_weight, lax.axis_size('tp')...  5.22 us
  transfers between devices with their start and end apart: 3, of which 2 were waited for; matrix products, arithmetic and copies ran while one was open for 13% of the time, Pallas kernels for 0%

profile of v1, /device:TPU:0, one launch (start us, length us, event | category | flops | bytes accessed | tf_op | source)
XLA Modules:
  0.0 145.0 jit_solution(16819453562813136352)
XLA Ops:
  6.5 0.0 copy-start
  6.5 0.0 all-gather.2.cloned.1.call-start
  6.5 0.7 all-gather.2.cloned.1.call-update
  7.3 1.6 %bitcast_dynamic-update-slice_fusion.7 = bf16[8,1,64,1024]{3,2,1,0:T(8,128)(2,1)} fusion(bf16[1,64,8192]{2,1,0:T(8,128)(2,1)} %param.9), kind=kLoop, calls=%fused_computation.16 | loop fusion | bytes 262144
  8.8 1.6 %bitcast_dynamic-update-slice_fusion.6 = bf16[8,1,64,1024]{3,2,1,0:T(8,128)(2,1)} fusion(bf16[8,1,64,1024]{3,2,1,0:T(8,128)(2,1)} %bitcast_dynamic-update-slice_fusion.7, bf16[1,64,8192]{2,1,0:T(8,128)(2,1)} %param.9), kind=kLoop, calls=%fused_computation.15 | loop fusion | bytes 262144
  10.4 1.6 %bitcast_dynamic-update-slice_fusion.5 = bf16[8,1,64,1024]{3,2,1,0:T(8,128)(2,1)} fusion(bf16[8,1,64,1024]{3,2,1,0:T(8,128)(2,1)} %bitcast_dynamic-update-slice_fusion.6, bf16[1,64,8192]{2,1,0:T(8,128)(2,1)} %param.9), kind=kLoop, calls=%fused_computation.14 | loop fusion | bytes 262144
  12.0 1.6 %bitcast_dynamic-update-slice_fusion.4 = bf16[8,1,64,1024]{3,2,1,0:T(8,128)(2,1)} fusion(bf16[8,1,64,1024]{3,2,1,0:T(8,128)(2,1)} %bitcast_dynamic-update-slice_fusion.5, bf16[1,64,8192]{2,1,0:T(8,128)(2,1)} %param.9), kind=kLoop, calls=%fused_computation.13 | loop fusion | bytes 262144
  13.5 1.6 %bitcast_dynamic-update-slice_fusion.3 = bf16[8,1,64,1024]{3,2,1,0:T(8,128)(2,1)} fusion(bf16[8,1,64,1024]{3,2,1,0:T(8,128)(2,1)} %bitcast_dynamic-update-slice_fusion.4, bf16[1,64,8192]{2,1,0:T(8,128)(2,1)} %param.9), kind=kLoop, calls=%fused_computation.12 | loop fusion | bytes 262144
  15.1 1.6 %bitcast_dynamic-update-slice_fusion.2 = bf16[8,1,64,1024]{3,2,1,0:T(8,128)(2,1)} fusion(bf16[8,1,64,1024]{3,2,1,0:T(8,128)(2,1)} %bitcast_dynamic-update-slice_fusion.3, bf16[1,64,8192]{2,1,0:T(8,128)(2,1)} %param.9), kind=kLoop, calls=%fused_computation.11 | loop fusion | bytes 262144
  16.7 1.6 %bitcast_dynamic-update-slice_fusion.1 = bf16[8,1,64,1024]{3,2,1,0:T(8,128)(2,1)} fusion(bf16[8,1,64,1024]{3,2,1,0:T(8,128)(2,1)} %bitcast_dynamic-update-slice_fusion.2, bf16[1,64,8192]{2,1,0:T(8,128)(2,1)} %param.9), kind=kLoop, calls=%fused_computation.10 | loop fusion | bytes 262144
  18.2 1.6 %bitcast_dynamic-update-slice_fusion = bf16[8,1,64,1024]{3,2,1,0:T(8,128)(2,1)} fusion(bf16[8,1,64,1024]{3,2,1,0:T(8,128)(2,1)} %bitcast_dynamic-update-slice_fusion.1, bf16[1,64,8192]{2,1,0:T(8,128)(2,1)} %param.9), kind=kLoop, calls=%fused_computation.9 | loop fusion | bytes 262144 | tf_op jit(solution)/shard_map/stack | solution.py:28
  19.8 5.2 %all-to-all-start = ((bf16[8,1,64,1024]{3,2,1,0:T(8,128)(2,1)}), bf16[8,1,64,1024]{3,2,1,0:T(8,128)(2,1)S(1)}, u32[]{:S(2)}, u32[]{:S(2)}) async-start(bf16[8,1,64,1024]{3,2,1,0:T(8,128)(2,1)} %bitcast_dynamic-update-slice_fusion), calls=%async_computation | async-start | bytes 2097152 | tf_op jit(solution)/shard_map/all_to_all | solution.py:27
  25.0 0.0 all-reduce.2.cloned.1.call-start
  25.1 0.9 select_reduce_fusion
  26.0 40.9 %all-gather.2.cloned.1.call-done = bf16[768,4096]{1,0:T(8,128)(2,1)} async-done(((bf16[768,512]{1,0:T(8,128)(2,1)}), bf16[768,4096]{1,0:T(8,128)(2,1)}) %all-gather.2.cloned.1.call-update) | async-done | bytes 6291472 | tf_op jit(solution)/shard_map/all_gather | solution.py:33
  66.9 0.0 copy-done
  66.9 5.4 %fusion.3 = bf16[6,64,128]{2,1,0:T(8,128)(2,1)} fusion(bf16[6,128,4096]{2,1,0:T(8,128)(2,1)} %bitcast.47, bf16[1,64,4096]{2,1,0:T(8,128)(2,1)S(1)} %copy-done, f32[6]{0:T(128)S(1)} %compare_convert_fusion), kind=kOutput, calls=%fused_computation.7 | convolution fusion | flops 402751488 | bytes 6914072 | tf_op jit(solution)/shard_map/btf,srf->bsrt/dot_general | solution.py:38
  72.3 0.0 all-reduce.2.cloned.1.call-update
  72.4 0.0 all-to-all-done
  72.4 0.6 gather_fusion
  73.0 51.6 %all-reduce.2.cloned.1.call-done = bf16[6,64,128]{2,1,0:T(8,128)(2,1)} async-done(((bf16[6,64,128]{2,1,0:T(8,128)(2,1)}), bf16[6,64,128]{2,1,0:T(8,128)(2,1)}) %all-reduce.2.cloned.1.call-update) | async-done | bytes 98320 | tf_op jit(solution)/shard_map/psum | solution.py:45
  124.6 1.5 %convolution_multiply_fusion = f32[6,128,1024]{2,1,0:T(8,128)S(1)} fusion(bf16[6,64,128]{2,1,0:T(8,128)(2,1)} %all-reduce.2.cloned.1.call-done, bf16[6,64,1024]{2,1,0:T(8,128)(2,1)S(1)} %gather_fusion), kind=kOutput, calls=%fused_computation.3 | convolution fusion | flops 101449728 | bytes 4030464 | tf_op jit(solution)/shard_map/brt,brc->btc/dot_general | solution.py:46
  126.1 12.1 %fusion = bf16[768,1024]{1,0:T(8,128)(2,1)} fusion(f32[6,128,1024]{2,1,0:T(8,128)S(1)} %convolution_multiply_fusion, bf16[768,4096]{1,0:T(8,128)(2,1)} %all-gather.2.cloned.1.call-done, bf16[4096,1024]{1,0:T(8,128)(2,1)} %param.7), kind=kOutput, calls=%fused_computation.2 | convolution fusion | flops 6444023808 | bytes 19398656 | tf_op jit(solution)/shard_map/dot_general | solution.py:34
  (3 shorter events, 0.0 us)
Async XLA Ops:
  6.5 60.4 %copy-start = (bf16[1,64,4096]{2,1,0:T(8,128)(2,1)S(1)}, bf16[1,64,4096]{2,1,0:T(8,128)(2,1)}, u32[]{:S(2)}) copy-start(bf16[1,64,4096]{2,1,0:T(8,128)(2,1)} %param.8) | copy-start | bytes 1572868
  6.5 60.4 %all-gather.2.cloned.1.call-start = ((), (), s32[]{:S(2)}) async-start(), calls=%async_computation.1 | async-start | bytes 7077888 | tf_op jit(solution)/shard_map/all_gather | solution.py:33
  19.8 52.6 %all-to-all-start = ((bf16[8,1,64,1024]{3,2,1,0:T(8,128)(2,1)}), bf16[8,1,64,1024]{3,2,1,0:T(8,128)(2,1)S(1)}, u32[]{:S(2)}, u32[]{:S(2)}) async-start(bf16[8,1,64,1024]{3,2,1,0:T(8,128)(2,1)} %bitcast_dynamic-update-slice_fusion), calls=%async_computation | async-start | bytes 2097152 | tf_op jit(solution)/shard_map/all_to_all | solution.py:27
  25.0 99.5 %all-reduce.2.cloned.1.call-start = ((), (), s32[]{:S(2)}) async-start(), calls=%async_computation.2 | async-start | bytes 196608 | tf_op jit(solution)/shard_map/psum | solution.py:45
Sparse Core Ops, SparseCore 0:
  9.2 57.6 all-gather.1
  72.5 52.0 all-reduce.1
